TPU v7x, 256 devices: a whole 4x4x8 slice. The times are simulated.
256 devices in a mesh: band: 16 (over y_lo, z), dom: 16 (over x, y_hi, core).
Axes of the slice: x: 4, y: 4 (y_hi: 2, y_lo: 2; y = y_hi * 2 + y_lo), z: 8, core: 2. Of those that a mesh axis runs over, the one named last changes fastest.
Arguments:
- wavefunctions: float32 [1024, 64, 16, 128], P('band', 'dom'), may hold values from -6 to 6
- potential: float32 [64, 16, 128], P('dom'), may hold values from -40 to 40
- projectors: float32 [64, 18, 4, 16, 128], P('dom'), may hold values from -0.0625 to 0.0625
- hamiltonian_correction: float32 [64, 18, 18], P('dom'), may hold values from -0.0390625 to 0.0390625
- delta_s: float32 [64, 18, 18], P('dom'), may hold values from -0.0390625 to 0.0390625
- projector_count: int32 [64], P('dom'), may hold values from 1 to 18
Outputs:
- ham: float32 [1024, 1024], P('band')
- correlation: float32 [1024, 1024], P('band')
All inputs are finite; a program needn't handle non-finite values.
Results may differ from a plain program's by a relative error of at most 0.00007.
Values sent between devices are 32-bit elements; how exact they have to be, the bound alone decides.
No kernel may reach another device: no remote copies, remote signals or barrier semaphores. Data moves between devices by JAX's collectives and lax.ppermute only.
A program may use at most 192 MiB of HBM per device.

v0:
```python
import jax
import jax.numpy as jnp
from jax import lax
from jax.sharding import PartitionSpec as P


def with_halo(cells, sides, width):
    for axis, dim in sides:
        count = lax.axis_size(axis)
        head = lax.slice_in_dim(cells, 0, width, axis=dim)
        tail = lax.slice_in_dim(cells, cells.shape[dim] - width, cells.shape[dim], axis=dim)
        cells = jnp.concatenate(
            [
                lax.ppermute(tail, axis, [(i, (i + 1) % count) for i in range(count)]),
                cells,
                lax.ppermute(head, axis, [((i + 1) % count, i) for i in range(count)]),
            ],
            axis=dim,
        )
    return cells


def side_by_side(arrays, axis, dim, along):
    columns = [a.reshape(*a.shape[:along], -1) for a in arrays]
    both = jnp.concatenate(columns, axis=along)
    result, at, finished = (lax.all_gather(both, axis, axis=dim, tiled=True), 0, [])
    for a, column in zip(arrays, columns):
        piece = result[..., at : at + column.shape[along]]
        finished.append(piece.reshape(*piece.shape[:along], *a.shape[along:]))
        at += column.shape[along]
    return tuple(finished)


def gathered_total(x, axis):
    return lax.all_gather(x, axis).sum(0)


def rows_product(left, right):
    return lax.dot_general(
        left,
        right,
        (((1,), (1,)), ((), ())),
        precision=lax.Precision.HIGHEST,
        preferred_element_type=jnp.float32,
    )


def kinetic_apply(padded, wavefn, potential):
    beside = padded[:, 2:] + padded[:, :-2]
    beside = beside + jnp.roll(wavefn, 1, 2) + jnp.roll(wavefn, -1, 2)
    beside = beside + jnp.roll(wavefn, 1, 3) + jnp.roll(wavefn, -1, 3)
    return 0.5 * (6.0 * wavefn - beside) + potential[None] * wavefn


def coefficients(flat_part, projector_flattened, slot_mask):
    return rows_product(flat_part, projector_flattened) * slot_mask[None, :]


def pair_blocks(own, piece_flat, piece_coef):
    hpsi_flat, psi_flat, coupled_h, coupled_s, volume = own
    ham_block = volume * rows_product(hpsi_flat, piece_flat) + rows_product(coupled_h, piece_coef)
    ovl_block = volume * rows_product(psi_flat, piece_flat) + rows_product(coupled_s, piece_coef)
    return (ham_block, ovl_block)


def place_blocks(blocks):
    ham_rows = blocks[0]
    ovl_rows = blocks[1]
    return (ham_rows, ovl_rows)


def on_device(
    wavefunctions, potential, projectors, hamiltonian_correction, delta_s, projector_count
):
    band_count, cx, ny, nz = wavefunctions.shape
    grid_cells = cx * ny * nz
    volume = 1.0 / (grid_cells * lax.axis_size("dom"))
    padded = with_halo(wavefunctions, (("dom", 1),), 1)
    hpsi = kinetic_apply(padded, wavefunctions, potential)
    psi_flat = wavefunctions.reshape(band_count, grid_cells)
    hpsi_flat = hpsi.reshape(band_count, grid_cells)
    atom_list = hamiltonian_correction.shape[0]
    slot_count = hamiltonian_correction.shape[1]
    slot_mask = (
        (jnp.arange(slot_count, dtype=jnp.int32)[None, :] < projector_count[:, None])
        .astype(jnp.float32)
        .reshape(-1)
    )
    projector_flattened = projectors.reshape(atom_list * slot_count, grid_cells)
    projector_coefficient = coefficients(psi_flat, projector_flattened, slot_mask)
    sym_h = 0.5 * (hamiltonian_correction + jnp.swapaxes(hamiltonian_correction, 1, 2))
    sym_s = 0.5 * (delta_s + jnp.swapaxes(delta_s, 1, 2))
    coefficient_triple = projector_coefficient.reshape(band_count, atom_list, slot_count)
    coupled_h = jnp.einsum(
        "bap,apq->baq", coefficient_triple, sym_h, precision=lax.Precision.HIGHEST
    ).reshape(band_count, -1)
    coupled_s = jnp.einsum(
        "bap,apq->baq", coefficient_triple, sym_s, precision=lax.Precision.HIGHEST
    ).reshape(band_count, -1)
    own = (hpsi_flat, psi_flat, coupled_h, coupled_s, volume)
    piece = side_by_side((wavefunctions, projector_coefficient), "band", 0, 1)
    rows = piece[0].shape[0]
    blocks = pair_blocks(own, piece[0].reshape(rows, grid_cells), piece[1])
    summed = place_blocks(blocks)
    reduced = (gathered_total(summed[0], "dom"), gathered_total(summed[1], "dom"))
    ham = reduced[0]
    correlation = reduced[1]
    return (ham, correlation)


def solution(mesh):
    placed = (
        P("band", "dom", None, None),
        P("dom", None, None),
        P("dom", None, None, None, None),
        P("dom", None, None),
        P("dom", None, None),
        P("dom"),
    )
    return jax.shard_map(
        on_device,
        mesh=mesh,
        in_specs=placed,
        out_specs=(P("band", None), P("band", None)),
        check_vma=False,
    )
```

profile of v0, /device:TPU:1, one launch (start us, length us, event | category | flops | bytes accessed | tf_op | source)
XLA Modules:
  0.0 554.7 jit_solution(8126949004628108999)
XLA Ops:
  7.2 0.0 copy-start.5
  7.2 0.0 copy-start
  7.2 0.0 all-gather.6.cloned.1.call-start
  7.2 3.5 reshape.44
  10.7 0.0 copy-done.5
  10.7 0.1 fusion.37
  10.8 0.1 reshape.48
  10.9 0.0 copy-done
  10.9 0.0 copy-start.1
  10.9 1.2 copy.36
  12.1 0.5 copy-done.1
  12.6 3.1 convolution_multiply_fusion
  15.7 1.5 pad_maximum_fusion
  17.2 0.0 copy-start.2
  17.2 0.0 all-gather.6.cloned.1.call-update
  17.2 0.0 all-gather.8.cloned.1.call-start
  17.2 1.1 fusion.42
  18.3 3.2 collective-permute-start
  21.5 1.1 collective-permute-start.1
  22.6 0.1 copy.15
  22.7 0.0 copy-done.2
  22.7 0.1 copy.14
  22.9 0.3 convolution_bitcast_fusion.1
  23.2 0.8 fusion.38
  24.0 0.8 fusion.39
  24.8 0.2 fusion.41
  25.0 0.0 copy-start.4
  25.0 0.5 fusion.40
  25.6 4.1 collective-permute-done
  29.7 5.0 collective-permute-done.1
  34.7 0.0 copy-done.4
  34.7 3.3 fusion.13
  38.0 342.0 %all-gather.6.cloned.1.call-done = f32[1024,8264]{1,0:T(8,128)} async-done(((f32[64,8264]{1,0:T(8,128)}), f32[1024,8264]{1,0:T(8,128)}) %all-gather.6.cloned.1.call-update) | async-done | bytes 33849360 | tf_op jit(solution)/shard_map/all_gather | solution.py:26
  380.0 1.8 fusion.31
  381.7 0.0 copy-start.3
  381.7 35.7 %fusion.19 = f32[64,1024]{1,0:T(8,128)} fusion(f32[64,1024]{1,0:T(8,128)S(1)} %fusion.31, f32[1024,8264]{1,0:T(8,128)} %all-gather.6.cloned.1.call-done, f32[8,8,64,128]{3,2,1,0:T(8,128)} %bitcast.48), kind=kOutput, calls=%fused_computation.20 | convolution fusion | flops 6442582016 | bytes 36175872 | tf_op jit(solution)/shard_map/dot_general | solution.py:39
  417.5 0.0 all-gather.8.cloned.1.call-update
  417.5 0.3 all-gather.10.cloned.1.call-start
  417.7 0.0 copy-done.3
  417.8 0.1 copy.17
  417.9 0.3 convolution_bitcast_fusion
  418.2 35.0 %fusion.27 = f32[64,1024]{1,0:T(8,128)S(1)} fusion(f32[1024,8264]{1,0:T(8,128)} %all-gather.6.cloned.1.call-done, f32[8,8,64,128]{3,2,1,0:T(8,128)S(1)} %bitcast.47), kind=kOutput, calls=%fused_computation.22 | convolution fusion | flops 6442516480 | bytes 35913728 | tf_op jit(solution)/shard_map/dot_general | solution.py:39
  453.2 2.5 convolution_add_fusion
  455.7 0.0 all-gather.10.cloned.1.call-update
  455.7 26.5 %all-gather.8.cloned.1.call-done = f32[1024,1024]{1,0:T(8,128)} async-done(((f32[64,1024]{1,0:T(8,128)}), f32[1024,1024]{1,0:T(8,128)}) %all-gather.8.cloned.1.call-update) | async-done | bytes 4194320 | tf_op jit(solution)/shard_map/all_gather | solution.py:35
  482.2 3.2 reduce_sum.18
  485.4 59.6 %all-gather.10.cloned.1.call-done = f32[1024,1024]{1,0:T(8,128)} async-done(((f32[64,1024]{1,0:T(8,128)}), f32[1024,1024]{1,0:T(8,128)}) %all-gather.10.cloned.1.call-update) | async-done | bytes 4194320 | tf_op jit(solution)/shard_map/all_gather | solution.py:35
  545.0 3.2 reduce_sum.19
  (5 shorter events, 0.0 us)
Async XLA Ops:
  7.2 3.6 copy-start.5
  7.2 3.7 copy-start
  7.2 372.8 %all-gather.6.cloned.1.call-start = ((), (), s32[]{:S(2)}) async-start(), calls=%async_computation | async-start | bytes 36208640 | tf_op jit(solution)/shard_map/all_gather | solution.py:26
  10.9 1.7 copy-start.1
  17.2 5.6 %copy-start.2 = (f32[4,18,18]{2,0,1:T(4,128)S(1)}, f32[4,18,18]{2,0,1:T(4,128)}, u32[]{:S(2)}) copy-start(f32[4,18,18]{2,0,1:T(4,128)} %param.9) | copy-start | bytes 15556
  17.2 465.0 %all-gather.8.cloned.1.call-start = ((), (), s32[]{:S(2)}) async-start(), calls=%async_computation.1 | async-start | bytes 4456448 | tf_op jit(solution)/shard_map/all_gather | solution.py:35
  18.3 11.4 %collective-permute-start = (f32[64,1,16,128]{3,2,1,0:T(8,128)}, f32[64,1,16,128]{3,2,1,0:T(8,128)S(1)}, u32[]{:S(2)}, u32[]{:S(2)}) collective-permute-start(f32[64,1,16,128]{3,2,1,0:T(8,128)} %get-tuple-element.10), channel_id=1, source_target_pairs={{1,0},{2,1},{3,2},{4,3},{5,4},{6,5},{7,6},{8,7},{9,8},{10,9},{11,1... | collective-permute-start | bytes 1572872 | tf_op jit(solution)/shard_map/ppermute | solution.py:16
  21.5 13.2 %collective-permute-start.1 = (f32[64,1,16,128]{3,2,1,0:T(8,128)}, f32[64,1,16,128]{3,2,1,0:T(8,128)S(1)}, u32[]{:S(2)}, u32[]{:S(2)}) collective-permute-start(f32[64,1,16,128]{3,2,1,0:T(8,128)} %get-tuple-element.11), channel_id=1, source_target_pairs={{0,1},{1,2},{2,3},{3,4},{4,5},{5,6},{6,7},{7,8},{8,9},{9,10},{10,1... | collective-permute-start | bytes 1572872 | tf_op jit(solution)/shard_map/ppermute | solution.py:14
  25.0 9.7 %copy-start.4 = (f32[4,16,128]{2,1,0:T(8,128)S(1)}, f32[4,16,128]{2,1,0:T(8,128)}, u32[]{:S(2)}) copy-start(f32[4,16,128]{2,1,0:T(8,128)} %param.7) | copy-start | bytes 98308
  381.7 36.0 %copy-start.3 = (f32[4,18,18]{2,0,1:T(4,128)S(1)}, f32[4,18,18]{2,0,1:T(4,128)}, u32[]{:S(2)}) copy-start(f32[4,18,18]{2,0,1:T(4,128)} %param.10) | copy-start | bytes 15556
  417.5 127.6 %all-gather.10.cloned.1.call-start = ((), (), s32[]{:S(2)}) async-start(), calls=%async_computation.2 | async-start | bytes 4456448 | tf_op jit(solution)/shard_map/all_gather | solution.py:35
Sparse Core Ops, SparseCore 0:
  17.3 362.6 all-gather.5
  417.6 64.5 all-gather.7
  484.9 60.0 all-gather.9
where the time goes:
time: 555 us
  waiting for transfers between devices  437 us (79%)
  matrix products  78.7 us (14%)
  between operations  13.9 us (3%)
  other arithmetic  11.3 us (2%)
  local copies, waits for them, and re-layouts  9.05 us (2%)
    all_gather x1, waiting for transfers between devices, side_by_side(): lax.all_gather(both, axis, axis=dim, tiled=True)  342 us
    all_gather x2, waiting for transfers between devices, gathered_total(): return lax.all_gather(x, axis).sum(0)  86.1 us
    dot_general x5, matrix products, rows_product(): lax.dot_general(left, right, (((1,), (1,)), ((), ())), precision=lax.Prec...  78.1 us
  transfers between devices with their start and end apart: 5, of which 5 were waited for; matrix products, arithmetic and copies ran while one was open for 9% of the time, Pallas kernels for 0%

commit v1 on v0

v1 whole, which is shorter than its diff:
```python
import jax
import jax.numpy as jnp
from jax import lax
from jax.experimental import pallas as pl
from jax.experimental.pallas import tpu as pltpu
from jax.sharding import PartitionSpec as P

F32 = jnp.float32
BF16 = jnp.bfloat16
HI = lax.Precision.HIGHEST
VMEM = pl.BlockSpec(memory_space=pltpu.VMEM)
SMEM = pl.BlockSpec(memory_space=pltpu.SMEM)
PARAMS = pltpu.CompilerParams(vmem_limit_bytes=56 * 1024 * 1024)

SLOT_LANES = (4, 28)


def lane_of(shape):
    return lax.broadcasted_iota(jnp.int32, shape, len(shape) - 1)


def spread_kernel(wf, coef, wh, ws, out):
    lane = lane_of((8, 128))
    block = lane // 8

    def body(bg, _):
        rows = pl.ds(pl.multiple_of(bg * 8, 8), 8)
        for x in range(4):
            v = [wf[pl.ds(bg * 512 + x * 16 + y, 8, stride=64), :] for y in range(16)]
            for s in (1, 2, 4, 8):
                low = (block & s) == 0
                nxt = list(v)
                for y in range(16):
                    if not y & s:
                        a, b = v[y], v[y + s]
                        nxt[y] = jnp.where(low, a, pltpu.roll(b, s * 8, 1))
                        nxt[y + s] = jnp.where(low, pltpu.roll(a, 128 - s * 8, 1), b)
                v = nxt
            for k in range(16):
                out[k, rows, x * 128 : (x + 1) * 128] = v[k]
        cs, hs, ss = coef[rows, :], wh[rows, :], ws[rows, :]
        for k in range(16):
            acc = jnp.zeros((8, 128), F32)
            for x in range(4):
                w = out[(k + 1) % 16, rows, x * 128 : (x + 1) * 128]
                acc = jnp.where(lane % 8 == x, pltpu.roll(w, x, 1) if x else w, acc)
            for first, at in ((4 * k, 4),) + (((64 + 4 * k, 28),) if k < 2 else ()):
                for t, a in enumerate((cs, hs, ss)):
                    to = at + 8 * t
                    here = (lane >= to) & (lane < to + 4)
                    acc = jnp.where(here, pltpu.roll(a, (to - first) % 128, 1), acc)
            out[k, rows, 512:640] = acc
        return 0

    lax.fori_loop(0, 8, body, 0)


def split(x):
    hi = x.astype(BF16)
    return hi, (x - hi.astype(F32)).astype(BF16)


def gram_kernel(core, r, xh, pot, keep, send, ah, al, ph, pll, eh, es, er, c, sd):
    cells = ah.shape[1]
    volume = 1.0 / (cells * 256)
    rows_per = 64
    lane = lane_of((rows_per, 128))
    slot = (lane % 8 >= 4) & ((lane < 8) | ((lane >= 28) & (lane < 32)))

    def prepare(i, _):
        rows = pl.ds(pl.multiple_of(i * rows_per, rows_per), rows_per)
        ext = r[rows, 512:640]
        for x in range(4):
            cols = slice(x * 128, (x + 1) * 128)
            p = r[rows, cols]
            beside = r[rows, (x + 1) * 128 : (x + 2) * 128] if x < 3 else xh[rows, :]
            beside = beside + pltpu.roll(p, 120, 1)
            zn = jnp.where(lane % 8 == 7, pltpu.roll(ext, 7 - x, 1), pltpu.roll(p, 127, 1))
            beside = beside + zn
            phi = (1.5 + 0.5 * pot[x : x + 1, :]) * p - 0.5 * beside
            ah[rows, cols], al[rows, cols] = split(p)
            ph[rows, cols], pll[rows, cols] = split(phi * volume)
        zero = jnp.zeros_like(ext)
        chi, clo = [a.astype(F32) for a in split(jnp.where(slot, ext, zero))]
        er[rows, :] = (chi + pltpu.roll(clo, 8, 1) + pltpu.roll(chi, 16, 1)).astype(BF16)
        for t, e in ((1, eh), (2, es)):
            hi, lo = [a.astype(F32) for a in split(jnp.where(slot, pltpu.roll(ext, 128 - 8 * t, 1), zero))]
            e[rows, :] = (hi + pltpu.roll(hi, 8, 1) + pltpu.roll(lo, 16, 1)).astype(BF16)
        return 0

    lax.fori_loop(0, 16, prepare, 0)

    def dot(a, b):
        return lax.dot_general(a, b, (((1,), (1,)), ((), ())), preferred_element_type=F32)

    def block(t, _):
        bi, bj = t // 4, t % 4
        ri = pl.ds(pl.multiple_of(bi * 256, 256), 256)
        rj = pl.ds(pl.multiple_of(bj * 256, 256), 256)

        def ham():
            acc = dot(ph[ri, :], ah[rj, :]) + dot(ph[ri, :], al[rj, :]) + dot(pll[ri, :], ah[rj, :])
            acc += dot(ah[ri, :], ph[rj, :]) + dot(al[ri, :], ph[rj, :]) + dot(ah[ri, :], pll[rj, :])
            return acc + dot(eh[ri, :], er[rj, :])

        def corr():
            acc = dot(ah[ri, :], ah[rj, :]) + dot(ah[ri, :], al[rj, :]) + dot(al[ri, :], ah[rj, :])
            return acc * volume + dot(es[ri, :], er[rj, :])

        @pl.when(bi < bj)
        def _():
            c[bi * 4 + bj] = ham()

        @pl.when(bi > bj)
        def _():
            c[bi * 4 + bj] = corr()

        @pl.when(bi == bj)
        def _():
            s = corr()
            sd[bi] = s
            g = lax.broadcasted_iota(jnp.int32, (256, 256), 0) // 64
            h = lax.broadcasted_iota(jnp.int32, (256, 256), 1) // 64
            c[bi * 4 + bj] = jnp.where(g <= h, ham(), s)

        return 0

    lax.fori_loop(0, 16, block, 0)

    low = lane < 64
    even_here = core[0] == 0

    def tile(g, h):
        return c[(g // 4) * 4 + h // 4, (g % 4) * 64 : (g % 4) * 64 + 64, (h % 4) * 64 : (h % 4) * 64 + 128]

    def own(g):
        at = (g % 4) * 64
        return sd[g // 4, at : at + 64, at // 128 * 128 : at // 128 * 128 + 128]

    def put(e, m, even, odd):
        keep[e, m] = jnp.where(even_here, even, odd)
        send[e, m] = jnp.where(even_here, odd, even)

    for e in range(8):
        for m in range(8):
            h0, h1 = (2 * e - 2 * m) % 16, (2 * e - 2 * m - 2) % 16
            t0, t1 = tile(2 * m, h0), tile(2 * m + 1, h0)
            even = jnp.where(low, t0, tile(2 * m + 1, h1))
            odd = pltpu.roll(jnp.where(low, t1, t0), 64, 1)
            put(e, m, even, odd)
        a, b = own(e), own(e + 8)
        if e % 2:
            a = pltpu.roll(a, 64, 1)
        else:
            b = pltpu.roll(b, 64, 1)
        extra = jnp.where(low, a, b)
        put(e, 8, extra, jnp.zeros_like(extra))


def rows_kernel(dom, parts, out, total):
    d = dom[0]
    low = lane_of((64, 128)) < 64
    for m in range(9):
        acc = parts[0, m]
        for s in range(1, 8):
            acc = acc + parts[s, m]
        total[m] = acc

    def swap(x):
        return pltpu.roll(x, 64, 1)

    for g in range(16):
        h = lax.rem(d - g + 16, 16)
        left = total[g // 2] if g % 2 == 0 else swap(total[g // 2])
        other = total[h // 2]
        right = jnp.where(h % 2 == 1, other, swap(other))
        own = total[8] if g >= 8 else swap(total[8])
        out[g] = jnp.where(low, left, jnp.where(h == g, own, right))


def finish_kernel(where, parts, out):
    b, h = where[0], where[1]
    t = parts[0]
    for s in range(1, 16):
        t = t + parts[s]
    low = lane_of((64, 128)) < 64
    flipped = jnp.concatenate([t, t], axis=0).T[64:, :]
    upper = jnp.where(low, t, flipped)
    lower = jnp.where(low, flipped, pltpu.roll(t, 64, 1))
    out[...] = jnp.where(b < h, upper, jnp.where(b > h, lower, t))


def assemble_kernel(band, parts, ham, corr):
    b = band[0]
    low = lane_of((64, 128)) < 64
    for j in range(8):
        t0 = parts[lax.rem(2 * j + b, 16)]
        t1 = parts[lax.rem(2 * j + 1 + b, 16)]
        cols = slice(j * 128, (j + 1) * 128)
        ham[:, cols] = jnp.where(low, t0, pltpu.roll(t1, 64, 1))
        corr[:, cols] = jnp.where(low, pltpu.roll(t0, 64, 1), t1)


def call(kernel, args, outs, scratch=(), flops=0):
    specs = [SMEM if a.dtype == jnp.int32 else VMEM for a in args]
    size = sum(a.size * 4 for a in args) + sum(o.size * 4 for o in outs)
    single = len(outs) == 1
    return pl.pallas_call(
        kernel,
        out_shape=outs[0] if single else outs,
        in_specs=specs,
        out_specs=VMEM if single else [VMEM] * len(outs),
        scratch_shapes=scratch,
        compiler_params=PARAMS,
        cost_estimate=pl.CostEstimate(flops=flops or size, bytes_accessed=size, transcendentals=0),
    )(*args)


def shape(*dims):
    return jax.ShapeDtypeStruct(dims, F32)


def rows_product(left, right):
    return lax.dot_general(left, right, (((1,), (1,)), ((), ())), precision=HI, preferred_element_type=F32)


def on_device(wavefunctions, potential, projectors, hamiltonian_correction, delta_s, projector_count):
    bands, cx, ny, nz = wavefunctions.shape
    atoms, slots = hamiltonian_correction.shape[:2]
    b, d = lax.axis_index("band"), lax.axis_index("dom")
    scalar = lambda *v: jnp.stack([jnp.asarray(x, jnp.int32) for x in v])

    mask = (jnp.arange(slots, dtype=jnp.int32)[None, :] < projector_count[:, None]).astype(F32).reshape(-1)
    proj = projectors.reshape(atoms * slots, cx * ny * nz)
    coef = rows_product(wavefunctions.reshape(bands, cx * ny * nz), proj) * mask[None, :]
    coef = jnp.pad(coef, ((0, 0), (0, 128 - atoms * slots)))

    def coupled(m):
        m = 0.5 * (m + jnp.swapaxes(m, 1, 2))
        full = jnp.eye(atoms, dtype=F32)[:, None, :, None] * m[:, :, None, :]
        full = full.reshape(atoms * slots, atoms * slots)
        full = jnp.pad(full, (0, 128 - atoms * slots))
        return jnp.dot(coef, full, precision=HI, preferred_element_type=F32)

    wh, ws = coupled(hamiltonian_correction), coupled(delta_s)
    parts = call(spread_kernel, (wavefunctions.reshape(bands * cx * ny, nz), coef, wh, ws), (shape(16, bands, 640),))
    slab = lax.all_to_all(parts, "band", 0, 0, tiled=True).reshape(16 * bands, 640)
    ahead = lax.ppermute(slab[:, :128], "dom", [((i + 1) % 16, i) for i in range(16)])
    pot = lax.dynamic_slice_in_dim(potential, b * 8, 8, 2).reshape(cx, ny * 8)
    m = 16 * bands
    keep, send = call(
        gram_kernel,
        (scalar(d % 2), slab, ahead, pot),
        (shape(8, 9, 64, 128), shape(8, 9, 64, 128)),
        [pltpu.VMEM((m, 512), BF16)] * 4
        + [pltpu.VMEM((m, 128), BF16)] * 3
        + [pltpu.VMEM((16, 256, 256), F32), pltpu.VMEM((4, 256, 256), F32)],
        flops=9 * 2 * m * m * 512,
    )
    mate = lax.ppermute(send, "dom", [(i, i ^ 1) for i in range(16)])
    groups = [[2 * e + c for e in range(8)] for c in range(2)]
    parts = lax.all_to_all(keep + mate, "dom", 0, 0, tiled=True, axis_index_groups=groups)
    parts = call(rows_kernel, (scalar(d), parts), (shape(16, 64, 128),), [pltpu.VMEM((9, 64, 128), F32)])
    parts = lax.all_to_all(parts, "band", 0, 0, tiled=True)
    own = call(finish_kernel, (scalar(b, (d - b + 16) % 16), parts), (shape(64, 128),))
    parts = lax.all_to_all(jnp.broadcast_to(own[None], (16, 64, 128)), "dom", 0, 0, tiled=True)
    return call(assemble_kernel, (scalar(b), parts), (shape(64, 1024), shape(64, 1024)))


def solution(mesh):
    placed = (
        P("band", "dom", None, None),
        P("dom", None, None),
        P("dom", None, None, None, None),
        P("dom", None, None),
        P("dom", None, None),
        P("dom"),
    )
    return jax.shard_map(
        on_device,
        mesh=mesh,
        in_specs=placed,
        out_specs=(P("band", None), P("band", None)),
        check_vma=False,
    )
```

time: 555 us -> 210 us (0.38)
  waiting for transfers between devices: 437 us -> 26.2 us
  blocking collectives: 0 us -> 124 us
  matrix products: 78.7 us -> 6.22 us
  Pallas kernels: 0 us -> 34.9 us
  between operations: 13.9 us -> 0.79 us
  other arithmetic: 11.3 us -> 2.94 us
    all_gather x3 -> x0, waiting for transfers between devices: 428 us -> none  [the longest x1 342 us: side_by_side(): lax.all_gather(both, axis, axis=dim, tiled=True)]
    all_to_all x0 -> x3, blocking collectives: none -> 124 us  [the longest x1 68.8 us: on_device(): lax.all_to_all(parts, 'band', 0, 0, tiled=True).reshape(16 * bands, 640)]
    dot_general x7 -> x3, matrix products: 78.7 us -> 6.22 us  [the longest x1 4.64 us: rows_product(): lax.dot_general(left, right, (((1,), (1,)), ((), ())), precision=HI, pref...]
    pallas_call x0 -> x5, Pallas kernels: none -> 34.9 us  [call(): pl.pallas_call(kernel, out_shape=outs[0] if single else outs, in_specs=sp...]
    all_to_all x0 -> x1, waiting for transfers between devices: none -> 12.7 us  [on_device(): parts = lax.all_to_all(parts, 'band', 0, 0, tiled=True)]
    reduce_sum x2 -> x0, other arithmetic: 6.37 us -> none  [gathered_total(): return lax.all_gather(x, axis).sum(0)]
  transfers between devices with their start and end apart: 5 -> 3, of which waited for: 5 -> 3; matrix products, arithmetic and copies ran while one was open for 9% -> 1% of each run, Pallas kernels for 0% -> 0%
where the time goes in v1:
time: 210 us; the launch traced here: 209 us
  blocking collectives  124 us (59%)
  Pallas kernels  34.9 us (17%)
  waiting for transfers between devices  26.2 us (12%)
  starting transfers between devices  8.42 us (4%)
  matrix products  6.22 us (3%)
  local copies, waits for them, and re-layouts  6.08 us (3%)
  other arithmetic  2.94 us (1%)
    all_to_all x1, blocking collectives, on_device(): lax.all_to_all(parts, 'band', 0, 0, tiled=True).reshape(16 * bands, 640)  68.8 us
    all_to_all x1, blocking collectives, on_device(): lax.all_to_all(keep + mate, 'dom', 0, 0, tiled=True, axis_index_groups=gr...  36.3 us
    pallas_call x5, Pallas kernels, call(): pl.pallas_call(kernel, out_shape=outs[0] if single else outs, in_specs=sp...  34.9 us
    all_to_all x1, blocking collectives, on_device(): lax.all_to_all(jnp.broadcast_to(own[None], (16, 64, 128)), 'dom', 0, 0, t...  18.4 us
    all_to_all x1, waiting for transfers between devices, on_device(): parts = lax.all_to_all(parts, 'band', 0, 0, tiled=True)  12.7 us
    ppermute x1, waiting for transfers between devices, on_device(): lax.ppermute(slab[:, :128], 'dom', [((i + 1) % 16, i) for i in range(16)])  8.73 us
    all_to_all x1, starting transfers between devices, on_device(): parts = lax.all_to_all(parts, 'band', 0, 0, tiled=True)  5.49 us
    ppermute x1, waiting for transfers between devices, on_device(): mate = lax.ppermute(send, 'dom', [(i, i ^ 1) for i in range(16)])  4.74 us
  transfers between devices with their start and end apart: 3, of which 3 were waited for; matrix products, arithmetic and copies ran while one was open for 1% of the time, Pallas kernels for 0%

profile of v1, /device:TPU:1, one launch (start us, length us, event | category | flops | bytes accessed | tf_op | source)
XLA Modules:
  0.0 209.1 jit_solution(11367322259576559863)
XLA Ops:
  0.6 0.0 copy-start
  0.7 0.0 copy-start.5
  0.7 0.0 copy-start.3
  0.7 0.0 copy-start.4
  0.7 2.5 %reshape.58 = f32[72,8192]{1,0:T(8,128)S(1)} reshape(f32[4,18,4,16,128]{4,3,2,1,0:T(8,128)} %param.8) | data formatting | bytes 4718592 | tf_op jit(solution)/shard_map/reshape | solution.py:234
  3.2 0.0 copy-done.5
  3.2 0.1 fusion.12
  3.3 0.1 reshape.61
  3.4 0.0 copy-done.3
  3.4 0.1 copy.12
  3.5 0.0 copy-done.4
  3.5 0.1 copy.14
  3.7 0.1 broadcast_multiply_fusion
  3.8 0.1 mul.61
  3.9 0.1 mul.57
  4.0 4.6 %fusion.3 = f32[64,72]{1,0:T(8,128)S(1)} fusion(f32[72,8192]{1,0:T(8,128)S(1)} %reshape.58, f32[8,8,64,128]{3,2,1,0:T(8,128)} %bitcast.24, f32[72]{0:T(128)S(1)} %reshape.61), kind=kOutput, calls=%fused_computation.3 | convolution fusion | flops 452989440 | bytes 4475168 | tf_op jit(solution)/shard_map/dot_general | solution.py:224
  8.7 0.8 fusion.6.ws
  9.5 0.8 fusion.8.wh
  10.3 0.6 pad.11.coef
  10.9 9.1 %shard_map.77 = f32[16,64,640]{2,1,0:T(8,128)} custom-call(f32[4096,128]{1,0:T(8,128)} %bitcast.25, f32[64,128]{1,0:T(8,128)} %pad.11.coef, f32[64,128]{1,0:T(8,128)} %fusion.8.wh, f32[64,128]{1,0:T(8,128)} %fusion.6.ws), custom_call_target="tpu_custom_call" | custom-call | flops 4816896 | bytes 4816896 | tf_op jit(solution)/shard_map/pallas_call | solution.py:208
  20.0 68.8 %all_to_all.20 = f32[16,64,640]{2,1,0:T(8,128)S(1)} all-to-all(f32[16,64,640]{2,1,0:T(8,128)} %shard_map.77), channel_id=1, replica_groups=mesh['band'=16,'dom'=16] {'band'}, dimensions={0} | all-to-all | bytes 5242880 | tf_op jit(solution)/shard_map/all_to_all | solution.py:247
  88.8 0.0 copy-start.1
  88.8 2.9 %collective-permute-start = (f32[1024,128]{1,0:T(8,128)S(1)}, f32[1024,128]{1,0:T(8,128)}, u32[]{:S(2)}, u32[]{:S(2)}) collective-permute-start(f32[1024,128]{1,0:T(8,128)S(1)} %slice.4), channel_id=1, source_target_pairs={{1,0},{2,1},{3,2},{4,3},{5,4},{6,5},{7,6},{8,7},{9,8},{10,9},{11,1... | collective-permute-start | bytes 1572872 | tf_op jit(solution)/shard_map/ppermute | solution.py:248
  91.7 0.0 copy-done
  91.8 0.1 constant_dynamic-slice_fusion
  91.8 0.7 reshape.60.pot
  92.5 8.7 %collective-permute-done.xh = f32[1024,128]{1,0:T(8,128)} collective-permute-done((f32[1024,128]{1,0:T(8,128)S(1)}, f32[1024,128]{1,0:T(8,128)}, u32[]{:S(2)}, u32[]{:S(2)}) %collective-permute-start) | collective-permute-done | bytes 524320 | tf_op jit(solution)/shard_map/ppermute | solution.py:248
  101.2 0.0 copy-done.1
  101.2 19.1 %shard_map.78 = (f32[8,9,64,128]{3,2,1,0:T(8,128)}, f32[8,9,64,128]{3,2,1,0:T(8,128)}) custom-call(s32[1]{0:T(128)} %bitcast.3.core, f32[1024,640]{1,0:T(8,128)} %bitcast.27, f32[1024,128]{1,0:T(8,128)} %collective-permute-done.xh, f32[4,128]{1,0:T(4,128)} %reshape.60.pot), custom_call_target="tpu_custom_call" | custom-call | flops 9663676416 | bytes 7866372 | tf_op jit(solution)/shard_map/pallas_call | solution.py:208
  120.4 0.0 collective-permute-start.1
  120.4 4.7 %collective-permute-done.1 = f32[8,9,64,128]{3,2,1,0:T(8,128)S(1)} collective-permute-done((f32[8,9,64,128]{3,2,1,0:T(8,128)}, f32[8,9,64,128]{3,2,1,0:T(8,128)S(1)}, u32[]{:S(2)}, u32[]{:S(2)}) %collective-permute-start.1) | collective-permute-done | bytes 2359328 | tf_op jit(solution)/shard_map/ppermute | solution.py:260
  125.1 2.1 %add.34 = f32[8,9,64,128]{3,2,1,0:T(8,128)S(1)} add(f32[8,9,64,128]{3,2,1,0:T(8,128)} %get-tuple-element.4, f32[8,9,64,128]{3,2,1,0:T(8,128)S(1)} %collective-permute-done.1) | non-fusion elementwise | flops 589824 | bytes 7077888 | tf_op jit(solution)/shard_map/add | solution.py:262
  127.2 36.3 %all_to_all.21.parts = f32[8,9,64,128]{3,2,1,0:T(8,128)} all-to-all(f32[8,9,64,128]{3,2,1,0:T(8,128)S(1)} %add.34), channel_id=1, replica_groups={{0,2,4,6,8,10,12,14},{1,3,5,7,9,11,13,15},{16,18,20,22,24,26,28,30},{17..., dimensions={0} | all-to-all | bytes 4718592 | tf_op jit(solution)/shard_map/all_to_all | solution.py:262
  163.5 2.9 %shard_map.79 = f32[16,64,128]{2,1,0:T(8,128)} custom-call(s32[1]{0:T(128)} %bitcast.2.dom, f32[8,9,64,128]{3,2,1,0:T(8,128)} %all_to_all.21.parts), custom_call_target="tpu_custom_call" | custom-call | flops 2883588 | bytes 2883588 | tf_op jit(solution)/shard_map/pallas_call | solution.py:208
  166.4 5.5 %all-to-all-start.2 = ((f32[16,64,128]{2,1,0:T(8,128)}), f32[16,64,128]{2,1,0:T(8,128)S(1)}, u32[]{:S(2)}, u32[]{:S(2)}) async-start(f32[16,64,128]{2,1,0:T(8,128)} %shard_map.79), calls=%async_computation.2 | async-start | bytes 1048576 | tf_op jit(solution)/shard_map/all_to_all | solution.py:264
  172.0 0.6 pad_add_fusion.where
  172.5 12.7 %all-to-all-done.2.parts = f32[16,64,128]{2,1,0:T(8,128)S(1)} async-done(((f32[16,64,128]{2,1,0:T(8,128)}), f32[16,64,128]{2,1,0:T(8,128)S(1)}, u32[]{:S(2)}, u32[]{:S(2)}) %all-to-all-start.2) | async-done | bytes 524320 | tf_op jit(solution)/shard_map/all_to_all | solution.py:264
  185.3 0.0 copy-start.2
  185.3 0.8 copy-done.2
  186.0 1.8 shard_map.80
  187.8 0.8 broadcast_in_dim.2
  188.6 18.4 %all_to_all.22.parts = f32[16,64,128]{2,1,0:T(8,128)} all-to-all(f32[16,64,128]{2,1,0:T(8,128)S(1)} %broadcast_in_dim.2), channel_id=1, replica_groups=mesh['band'=16,'dom'=16] {'dom'}, dimensions={0} | all-to-all | bytes 1048576 | tf_op jit(solution)/shard_map/all_to_all | solution.py:266
  207.0 2.0 shard_map.81
  (6 shorter events, 0.1 us)
Async XLA Ops:
  0.6 91.1 %copy-start = (f32[4,16,128]{2,1,0:T(8,128)S(1)}, f32[4,16,128]{2,1,0:T(8,128)}, u32[]{:S(2)}) copy-start(f32[4,16,128]{2,1,0:T(8,128)} %param.7) | copy-start | bytes 98308
  0.7 2.5 %copy-start.5 = (s32[4]{0:T(128)S(1)}, s32[4]{0:T(128)}, u32[]{:S(2)}) copy-start(s32[4]{0:T(128)} %param.11) | copy-start | bytes 52
  0.7 2.7 %copy-start.3 = (f32[4,18,18]{2,0,1:T(4,128)S(1)}, f32[4,18,18]{2,0,1:T(4,128)}, u32[]{:S(2)}) copy-start(f32[4,18,18]{2,0,1:T(4,128)} %param.9) | copy-start | bytes 15556
  0.7 2.8 %copy-start.4 = (f32[4,18,18]{2,0,1:T(4,128)S(1)}, f32[4,18,18]{2,0,1:T(4,128)}, u32[]{:S(2)}) copy-start(f32[4,18,18]{2,0,1:T(4,128)} %param.10) | copy-start | bytes 15556
  88.8 12.4 %copy-start.1 = (f32[16,64,640]{2,1,0:T(8,128)}, f32[16,64,640]{2,1,0:T(8,128)S(1)}, u32[]{:S(2)}) copy-start(f32[16,64,640]{2,1,0:T(8,128)S(1)} %all_to_all.20) | copy-start | bytes 7864324
  88.8 12.4 %collective-permute-start = (f32[1024,128]{1,0:T(8,128)S(1)}, f32[1024,128]{1,0:T(8,128)}, u32[]{:S(2)}, u32[]{:S(2)}) collective-permute-start(f32[1024,128]{1,0:T(8,128)S(1)} %slice.4), channel_id=1, source_target_pairs={{1,0},{2,1},{3,2},{4,3},{5,4},{6,5},{7,6},{8,7},{9,8},{10,9},{11,1... | collective-permute-start | bytes 1572872 | tf_op jit(solution)/shard_map/ppermute | solution.py:248
  120.4 4.7 %collective-permute-start.1 = (f32[8,9,64,128]{3,2,1,0:T(8,128)}, f32[8,9,64,128]{3,2,1,0:T(8,128)S(1)}, u32[]{:S(2)}, u32[]{:S(2)}) collective-permute-start(f32[8,9,64,128]{3,2,1,0:T(8,128)} %get-tuple-element.5), channel_id=1, source_target_pairs={{0,1},{1,0},{2,3},{3,2},{4,5},{5,4},{6,7},{7,6},{8,9},{9,8},{10,11... | collective-permute-start | bytes 7077896 | tf_op jit(solution)/shard_map/ppermute | solution.py:260
  166.4 18.8 %all-to-all-start.2 = ((f32[16,64,128]{2,1,0:T(8,128)}), f32[16,64,128]{2,1,0:T(8,128)S(1)}, u32[]{:S(2)}, u32[]{:S(2)}) async-start(f32[16,64,128]{2,1,0:T(8,128)} %shard_map.79), calls=%async_computation.2 | async-start | bytes 1048576 | tf_op jit(solution)/shard_map/all_to_all | solution.py:264
  185.3 0.8 copy-start.2
